TPU v7x, 256 devices: a whole 4x4x8 slice. The times are simulated.
256 devices in a mesh: blk: 128 (over z, x, y_lo, core), rep: 2 (over y_hi).
Axes of the slice: x: 4, y: 4 (y_hi: 2, y_lo: 2; y = y_hi * 2 + y_lo), z: 8, core: 2. Of those that a mesh axis runs over, the one named last changes fastest.
Arguments:
- particles: bfloat16 [7168, 2048], P(('blk', 'rep')), may hold values from -0.0029907227 to 0.0029907227
- scores: bfloat16 [7168, 2048], P(('blk', 'rep')), may hold values from -60 to 60, as said below
- spread: float32 [1], replicated, may hold values from 0.00034816 to 0.00069632
Outputs:
- direction: float32 [7168, 2048], P(('blk', 'rep'))
Inputs may be any that keep to these rules, and one draw needn't show every extreme that they name: `scores`: scores of the particles' log posterior.
All inputs are finite; a program needn't handle non-finite values.
Results may differ from a plain program's by a relative error of at most 0.0003.
Values may be sent and summed in bfloat16 or wider, within the bound.
No kernel may reach another device: no remote copies, remote signals or barrier semaphores. Data moves between devices by JAX's collectives and lax.ppermute only.
A program may use at most 128 MiB of HBM per device.

v0:
```python
import jax
import jax.numpy as jnp
from jax import lax
from jax.sharding import PartitionSpec as P


def sent_to_all(value, axis):
    count = lax.axis_size(axis)
    return lax.all_to_all(
        jnp.broadcast_to(value[None], (count, *value.shape)), axis, 0, 0, tiled=True
    )


def joined_along(blocks, dim):
    dims = list(blocks.shape[1:])
    dims[dim] *= blocks.shape[0]
    return jnp.moveaxis(blocks, 0, dim).reshape(dims)


def gather_directly(value, axis, dim):
    blocks = sent_to_all(value, axis)
    return joined_along(blocks, dim)


def in_blocks(value, dim, count):
    before, after = (value.shape[:dim], value.shape[dim + 1 :])
    return jnp.moveaxis(value.reshape(*before, count, -1, *after), dim, 0)


def summed_on_arrival(value, axis, dim):
    blocks = in_blocks(value, dim, lax.axis_size(axis))
    arrived = lax.all_to_all(blocks, axis, split_axis=0, concat_axis=0, tiled=True)
    return arrived.sum(axis=0)


def kernel_weights(targets, target_norm, source_x, inverse):
    cross_dots = lax.dot_general(
        targets, source_x, (((1,), (1,)), ((), ())), preferred_element_type=jnp.float32
    )
    source_wide = source_x.astype(jnp.float32)
    source_norm = jnp.sum(source_wide * source_wide, axis=1)
    squared = jnp.maximum(target_norm[:, None] + source_norm[None, :] - 2.0 * cross_dots, 0.0)
    return jnp.exp(-squared * inverse)


def shards(particles, scores, spread):
    inverse = 1.0 / spread[0]
    own_count = particles.shape[0]
    population = own_count * lax.axis_size("blk") * lax.axis_size("rep")
    targets = gather_directly(particles, "rep", 0)
    target_wide = targets.astype(jnp.float32)
    target_norm = jnp.sum(target_wide * target_wide, axis=1)
    stacked = jnp.stack([scores, particles], axis=0)
    source = lax.all_gather(stacked, "blk", axis=1, tiled=True)
    weights = kernel_weights(targets, target_norm, source[1], inverse)
    weights_low = weights.astype(jnp.bfloat16)
    combined_step = jnp.einsum(
        "ij,cjd->cid", weights_low, source, preferred_element_type=jnp.float32
    )
    row_total = jnp.sum(weights, axis=1)
    drive_sum = combined_step[0]
    pull_sum = combined_step[1]
    partial_value = (
        drive_sum + 2.0 * inverse * (target_wide * row_total[:, None] - pull_sum)
    ) / population
    return summed_on_arrival(partial_value, "rep", 0)


def solution(mesh):
    return jax.shard_map(
        shards,
        mesh=mesh,
        in_specs=(P(("blk", "rep"), None), P(("blk", "rep"), None), P()),
        out_specs=P(("blk", "rep"), None),
        check_vma=False,
    )
```

profile of v0, /device:TPU:32, one launch (start us, length us, event | category | flops | bytes accessed | tf_op | source)
XLA Modules:
  0.0 333.5 jit_solution(15019230798505263982)
XLA Ops:
  6.5 0.0 all-gather.2.cloned.1.call-start
  6.5 1.0 pad_maximum_fusion
  7.5 0.9 copy.5
  8.5 0.0 all-gather.2.cloned.1.call-update
  8.5 1.6 broadcast_in_dim.2
  10.1 4.5 %all-to-all-start = ((bf16[2,28,2048]{2,1,0:T(8,128)(2,1)}), bf16[2,28,2048]{2,1,0:T(8,128)(2,1)S(1)}, u32[]{:S(2)}, u32[]{:S(2)}) async-start(bf16[2,28,2048]{2,1,0:T(8,128)(2,1)} %broadcast_in_dim.2), calls=%async_computation | async-start | bytes 524288 | tf_op jit(solution)/shard_map/all_to_all | solution.py:9
  15.3 6.0 %all-to-all-done = bf16[2,28,2048]{2,1,0:T(8,128)(2,1)S(1)} async-done(((bf16[2,28,2048]{2,1,0:T(8,128)(2,1)}), bf16[2,28,2048]{2,1,0:T(8,128)(2,1)S(1)}, u32[]{:S(2)}, u32[]{:S(2)}) %all-to-all-start) | async-done | bytes 229408 | tf_op jit(solution)/shard_map/all_to_all | solution.py:9
  21.3 0.1 fusion.8
  21.4 0.1 add.19
  21.5 0.1 reshape.19
  21.5 235.9 %all-gather.2.cloned.1.call-done = bf16[2,3584,2048]{2,0,1:T(2,128)(2,1)} async-done(((bf16[2,28,2048]{2,0,1:T(2,128)(2,1)}), bf16[2,3584,2048]{2,0,1:T(2,128)(2,1)}) %all-gather.2.cloned.1.call-update) | async-done | bytes 29360144 | tf_op jit(solution)/shard_map/all_gather | solution.py:54
  257.4 20.5 %copy.7 = bf16[2,3584,2048]{2,1,0:T(8,128)(2,1)} copy(bf16[2,3584,2048]{2,0,1:T(2,128)(2,1)} %all-gather.2.cloned.1.call-done) | data formatting | bytes 58720256 | tf_op jit(solution)/shard_map/all_gather | solution.py:54
  277.9 8.1 %multiply_reduce_fusion = f32[3584]{0:T(1024)S(1)} fusion(bf16[2,3584,2048]{2,1,0:T(8,128)(2,1)} %copy.7), kind=kLoop, calls=%fused_computation | loop fusion | flops 22016512 | bytes 14694400 | tf_op jit(solution)/shard_map/reduce_sum | solution.py:41
  286.0 8.2 %fusion.17 = (f32[56]{0:T(128)S(1)}, bf16[56,3584]{1,0:T(8,128)(2,1)S(1)}) fusion(f32[]{:T(128)} %bitcast.4, bf16[56,2048]{1,0:T(8,128)(2,1)S(1)} %reshape.19, bf16[2,3584,2048]{2,1,0:T(8,128)(2,1)} %copy.7, f32[3584]{0:T(1024)S(1)} %multiply_reduce_fusion, f32[56]{0:T(128)S(1)} %add.19), kind=kOutput, calls=%fused_computation.23 | convolution fusion | flops 823689152 | bytes 15326144 | tf_op jit(solution)/shard_map/dot_general | solution.py:37
  294.2 18.1 %convolution_bitcast_fusion = f32[2,56,2048]{2,1,0:T(8,128)S(1)} fusion(bf16[56,3584]{1,0:T(8,128)(2,1)S(1)} %get-tuple-element.8, bf16[2,3584,2048]{2,0,1:T(2,128)(2,1)} %all-gather.2.cloned.1.call-done), kind=kOutput, calls=%fused_computation.10 | convolution fusion | flops 1644167168 | bytes 30679040 | tf_op jit(solution)/shard_map/ij,cjd->cid/dot_general | solution.py:57
  312.4 0.1 fusion.16
  312.5 0.1 mul.52
  312.6 0.2 fusion.12
  312.8 13.1 %all_to_all.10 = f32[2,28,2048]{2,1,0:T(8,128)S(1)} all-to-all(f32[2,28,2048]{2,1,0:T(8,128)S(1)} %fusion.12), channel_id=1, replica_groups=mesh['blk'=128,'rep'=2] {'rep'}, dimensions={0} | all-to-all | bytes 917504 | tf_op jit(solution)/shard_map/all_to_all | solution.py:32
  325.9 0.7 reduce_sum.39
  (2 shorter events, 0.1 us)
Async XLA Ops:
  6.5 250.9 %all-gather.2.cloned.1.call-start = ((), (), s32[]{:S(2)}) async-start(), calls=%async_computation.2 | async-start | bytes 29589504 | tf_op jit(solution)/shard_map/all_gather | solution.py:54
  10.1 11.1 %all-to-all-start = ((bf16[2,28,2048]{2,1,0:T(8,128)(2,1)}), bf16[2,28,2048]{2,1,0:T(8,128)(2,1)S(1)}, u32[]{:S(2)}, u32[]{:S(2)}) async-start(bf16[2,28,2048]{2,1,0:T(8,128)(2,1)} %broadcast_in_dim.2), calls=%async_computation | async-start | bytes 524288 | tf_op jit(solution)/shard_map/all_to_all | solution.py:9
Sparse Core Ops, SparseCore 0:
  9.2 248.1 all-gather.1
where the time goes:
time: 334 us
  waiting for transfers between devices  242 us (72%)
  matrix products  26.3 us (8%)
  local copies, waits for them, and re-layouts  23.5 us (7%)
  between operations  14.1 us (4%)
  blocking collectives  13.1 us (4%)
  other arithmetic  10.1 us (3%)
  starting transfers between devices  4.46 us (1%)
    all_gather x1, waiting for transfers between devices, shards(): source = lax.all_gather(stacked, 'blk', axis=1, tiled=True)  236 us
    all_gather x1, local copies, waits for them, and re-layouts, shards(): source = lax.all_gather(stacked, 'blk', axis=1, tiled=True)  20.5 us
    dot_general x1, matrix products, shards(): jnp.einsum('ij,cjd->cid', weights_low, source, preferred_element_type=jnp...  18.1 us
    all_to_all x1, blocking collectives, summed_on_arrival(): lax.all_to_all(blocks, axis, split_axis=0, concat_axis=0, tiled=True)  13.1 us
    dot_general x1, matrix products, kernel_weights(): lax.dot_general(targets, source_x, (((1,), (1,)), ((), ())), preferred_el...  8.21 us
    reduce_sum x1, other arithmetic, kernel_weights(): source_norm = jnp.sum(source_wide * source_wide, axis=1)  8.09 us
  transfers between devices with their start and end apart: 2, of which 2 were waited for; matrix products, arithmetic and copies ran while one was open for 1% of the time, Pallas kernels for 0%

commit v1 on v0

--- a/solution.py
+++ b/solution.py
@@ -51,7 +51,9 @@
     target_wide = targets.astype(jnp.float32)
     target_norm = jnp.sum(target_wide * target_wide, axis=1)
     stacked = jnp.stack([scores, particles], axis=0)
-    source = lax.all_gather(stacked, "blk", axis=1, tiled=True)
+    source = jnp.concatenate(
+        lax.all_to_all(jnp.stack([stacked] * lax.axis_size("blk")), "blk", 0, 0), axis=1
+    )
     weights = kernel_weights(targets, target_norm, source[1], inverse)
     weights_low = weights.astype(jnp.bfloat16)
     combined_step = jnp.einsum(

time: 334 us -> 930 us (2.78)
  waiting for transfers between devices: 242 us -> 671 us
  local copies, waits for them, and re-layouts: 23.5 us -> 137 us
  other arithmetic: 10.1 us -> 56.8 us
  between operations: 14.1 us -> 0.76 us
  starting transfers between devices: 4.46 us -> 17.5 us
    all_to_all x0 -> x1, waiting for transfers between devices: none -> 666 us  [shards(): lax.all_to_all(jnp.stack([stacked] * lax.axis_size('blk')), 'blk', 0, 0)]
    all_gather x1 -> x0, waiting for transfers between devices: 236 us -> none  [shards(): source = lax.all_gather(stacked, 'blk', axis=1, tiled=True)]
    slice x0 -> x1, local copies, waits for them, and re-layouts: none -> 97.2 us  [shards(): weights = kernel_weights(targets, target_norm, source[1], inverse)]
    reduce_sum x1, other arithmetic: 8.09 us -> 54.7 us  [kernel_weights(): source_norm = jnp.sum(source_wide * source_wide, axis=1)]
    squeeze x0 -> x1, local copies, waits for them, and re-layouts: none -> 20.6 us  [shards(): weights = kernel_weights(targets, target_norm, source[1], inverse)]
    all_gather x1 -> x0, local copies, waits for them, and re-layouts: 20.5 us -> none  [shards(): source = lax.all_gather(stacked, 'blk', axis=1, tiled=True)]
    another operation x0 -> x1, local copies, waits for them, and re-layouts: none -> 17.3 us  [shards(): jnp.stack([stacked] * lax.axis_size('blk'))]
    all_to_all x0 -> x1, starting transfers between devices: none -> 13 us  [shards(): lax.all_to_all(jnp.stack([stacked] * lax.axis_size('blk')), 'blk', 0, 0)]
  transfers between devices with their start and end apart: 2 -> 2, of which waited for: 2 -> 2; matrix products, arithmetic and copies ran while one was open for 1% -> 0% of each run, Pallas kernels for 0% -> 0%
where the time goes in v1:
time: 930 us; the launch traced here: 924 us
  waiting for transfers between devices  671 us (72%)
  local copies, waits for them, and re-layouts  137 us (15%)
  other arithmetic  56.8 us (6%)
  matrix products  28.1 us (3%)
  starting transfers between devices  17.5 us (2%)
  blocking collectives  11.9 us (1%)
    all_to_all x1, waiting for transfers between devices, shards(): lax.all_to_all(jnp.stack([stacked] * lax.axis_size('blk')), 'blk', 0, 0)  666 us
    slice x1, local copies, waits for them, and re-layouts, shards(): weights = kernel_weights(targets, target_norm, source[1], inverse)  97.2 us
    reduce_sum x1, other arithmetic, kernel_weights(): source_norm = jnp.sum(source_wide * source_wide, axis=1)  54.7 us
    squeeze x1, local copies, waits for them, and re-layouts, shards(): weights = kernel_weights(targets, target_norm, source[1], inverse)  20.6 us
  transfers between devices with their start and end apart: 2, of which 2 were waited for; matrix products, arithmetic and copies ran while one was open for 0% of the time, Pallas kernels for 0%

profile of v1, /device:TPU:32, one launch (start us, length us, event | category | flops | bytes accessed | tf_op | source)
XLA Modules:
  0.0 923.7 jit_solution(2775050105584541709)
XLA Ops:
  0.0 1.6 broadcast_in_dim.2
  1.6 4.5 all-to-all-start.1
  6.1 1.0 pad_maximum_fusion
  7.1 0.2 copy.6
  7.3 5.4 all-to-all-done.1
  12.8 17.3 %stack.11 = bf16[128,2,28,2048]{3,1,2,0:T(2,128)(2,1)} broadcast(bf16[2,28,2048]{2,0,1:T(2,128)(2,1)S(1)} %copy.6), dimensions={1,2,3} | broadcast | bytes 29589504 | tf_op jit(solution)/shard_map/stack | solution.py:55
  30.1 13.0 %all-to-all-start = ((bf16[128,2,28,2048]{3,1,2,0:T(2,128)(2,1)}), bf16[128,2,28,2048]{3,1,2,0:T(2,128)(2,1)}, u32[]{:S(2)}, u32[]{:S(2)}) async-start(bf16[128,2,28,2048]{3,1,2,0:T(2,128)(2,1)} %stack.11), calls=%async_computation | async-start | bytes 58720256 | tf_op jit(solution)/shard_map/all_to_all | solution.py:55
  43.8 0.1 fusion.11
  44.0 0.1 add.21
  44.0 0.1 reshape.33
  44.1 666.0 %all-to-all-done = bf16[128,2,28,2048]{3,1,2,0:T(2,128)(2,1)} async-done(((bf16[128,2,28,2048]{3,1,2,0:T(2,128)(2,1)}), bf16[128,2,28,2048]{3,1,2,0:T(2,128)(2,1)}, u32[]{:S(2)}, u32[]{:S(2)}) %all-to-all-start) | async-done | bytes 29360160 | tf_op jit(solution)/shard_map/all_to_all | solution.py:55
  710.1 97.2 %slice_reduce_fusion = bf16[128,28,2048]{2,1,0:T(8,128)(2,1)} fusion(bf16[2,128,28,2048]{3,0,2,1:T(2,128)(2,1)} %bitcast.2), kind=kLoop, calls=%fused_computation.3 | loop fusion | bytes 29360128 | tf_op jit(solution)/shard_map/slice | solution.py:57
  807.2 54.7 %multiply_reduce_fusion = f32[128,28]{1,0:T(8,128)S(1)} fusion(bf16[2,128,28,2048]{3,0,2,1:T(2,128)(2,1)} %bitcast.2), kind=kLoop, calls=%fused_computation.2 | loop fusion | flops 22016512 | bytes 14694400 | tf_op jit(solution)/shard_map/reduce_sum | solution.py:41
  861.9 20.6 %squeeze.10 = bf16[3584,2048]{1,0:T(8,128)(2,1)} reshape(bf16[128,28,2048]{2,1,0:T(8,128)(2,1)} %slice_reduce_fusion) | data formatting | bytes 29360128 | tf_op jit(solution)/shard_map/squeeze | solution.py:57
  882.5 0.1 add.23
  882.6 9.9 %fusion.19 = (f32[56]{0:T(128)S(1)}, bf16[56,3584]{1,0:T(8,128)(2,1)S(1)}) fusion(f32[]{:T(128)} %bitcast.5, bf16[3584,2048]{1,0:T(8,128)(2,1)} %squeeze.10, bf16[56,2048]{1,0:T(8,128)(2,1)S(1)} %reshape.33, f32[3584]{0:T(1024)S(1)} %add.23, f32[56]{0:T(128)S(1)} %add.21), kind=kOutput, calls=%fused_computation.23 | convolution fusion | flops 823689152 | bytes 15325636 | tf_op jit(solution)/shard_map/dot_general | solution.py:37
  892.5 18.2 %fusion.8 = f32[2,56,2048]{2,1,0:T(8,128)S(1)} fusion(bf16[2,3584,2048]{2,0,1:T(2,128)(2,1)} %bitcast.3, bf16[56,3584]{1,0:T(8,128)(2,1)S(1)} %get-tuple-element.8), kind=kOutput, calls=%fused_computation.11 | convolution fusion | flops 1644167168 | bytes 30679040 | tf_op jit(solution)/shard_map/ij,cjd->cid/dot_general | solution.py:59
  910.7 0.1 fusion.18
  910.9 0.1 mul.53
  910.9 0.2 fusion.15
  911.1 11.9 %all_to_all.15 = f32[2,28,2048]{2,1,0:T(8,128)S(1)} all-to-all(f32[2,28,2048]{2,1,0:T(8,128)S(1)} %fusion.15), channel_id=1, replica_groups=mesh['blk'=128,'rep'=2] {'rep'}, dimensions={0} | all-to-all | bytes 917504 | tf_op jit(solution)/shard_map/all_to_all | solution.py:32
  923.0 0.7 reduce_sum.39
  (2 shorter events, 0.1 us)
Async XLA Ops:
  1.6 11.1 %all-to-all-start.1 = ((bf16[2,28,2048]{2,1,0:T(8,128)(2,1)}), bf16[2,28,2048]{2,1,0:T(8,128)(2,1)S(1)}, u32[]{:S(2)}, u32[]{:S(2)}) async-start(bf16[2,28,2048]{2,1,0:T(8,128)(2,1)} %broadcast_in_dim.2), calls=%async_computation.1 | async-start | bytes 524288 | tf_op jit(solution)/shard_map/all_to_all | solution.py:9
  30.1 680.0 %all-to-all-start = ((bf16[128,2,28,2048]{3,1,2,0:T(2,128)(2,1)}), bf16[128,2,28,2048]{3,1,2,0:T(2,128)(2,1)}, u32[]{:S(2)}, u32[]{:S(2)}) async-start(bf16[128,2,28,2048]{3,1,2,0:T(2,128)(2,1)} %stack.11), calls=%async_computation | async-start | bytes 58720256 | tf_op jit(solution)/shard_map/all_to_all | solution.py:55
